TPU v7x, 128 devices: a whole 4x4x4 slice. The times are simulated.
128 devices in a mesh: row: 8 (over x_hi, z), col: 16 (over x_lo, y, core).
Axes of the slice: x: 4 (x_hi: 2, x_lo: 2; x = x_hi * 2 + x_lo), y: 4, z: 4, core: 2. Of those that a mesh axis runs over, the one named last changes fastest.
Arguments:
- features: bfloat16 [384, 256, 512], P('row', 'col'), may hold values from -12 to 12
- cotangent: bfloat16 [384, 256, 512], P('row', 'col'), may hold values from -6 to 6
- w_query: bfloat16 [512, 512], replicated, may hold values from -0.53033009 to 0.53033009
- w_key: bfloat16 [512, 512], replicated, may hold values from -0.53033009 to 0.53033009
- w_value: bfloat16 [512, 512], replicated, may hold values from -0.25 to 0.25
- w_out: bfloat16 [512, 512], replicated, may hold values from -0.25 to 0.25
Outputs:
- layer_out: bfloat16 [384, 256, 512], P('row', 'col')
- grad_features: bfloat16 [384, 256, 512], P('row', 'col')
- grad_query: float32 [512, 512], replicated
- grad_key: float32 [512, 512], replicated
- grad_value: float32 [512, 512], replicated
- grad_proj: float32 [512, 512], replicated
All inputs are finite; a program needn't handle non-finite values.
Results may differ from a plain program's by a relative error of at most 0.012.
The roundings to bfloat16 on the way count: a program that leaves them out, or rounds other values in their place, can miss the bound.
Values may be sent and summed in bfloat16 or wider, within the bound.
A program may use at most 128 MiB of HBM per device.

v0:
```python
import jax
import jax.numpy as jnp
from jax import lax
from jax.sharding import PartitionSpec as P

HEADS = 8


NEG_FILL = -1e30


def passed_along(block, axis, distance):
    devices = range(lax.axis_size(axis))
    route = [((i - distance) % len(devices), i) for i in devices]
    return lax.ppermute(block, axis, route)


def sent_together(arrays, axis, dim, along):
    both = jnp.concatenate(arrays, axis=along)
    filled, at, finished = (lax.all_gather(both, axis, axis=dim, tiled=True), 0, [])
    for a in arrays:
        finished.append(lax.slice_in_dim(filled, at, at + a.shape[along], axis=along))
        at += a.shape[along]
    return tuple(finished)


def product_of(form, left, right):
    return jnp.einsum(form, left, right, preferred_element_type=jnp.float32)


def project(left, weight):
    return jnp.dot(left, weight, preferred_element_type=jnp.float32).astype(jnp.bfloat16)


def times_transposed(left, weight):
    return lax.dot_general(
        left, weight, (((1,), (1,)), ((), ())), preferred_element_type=jnp.float32
    )


def inner_sum(left, right):
    return lax.dot_general(
        left, right, (((0,), (0,)), ((), ())), preferred_element_type=jnp.float32
    )


def inner_exact(left, right):
    return lax.dot_general(
        left,
        right,
        (((0,), (0,)), ((), ())),
        precision=lax.Precision.HIGHEST,
        preferred_element_type=jnp.float32,
    )


def transposed_exact(left, weight):
    return lax.dot_general(
        left,
        weight.astype(jnp.float32),
        (((1,), (1,)), ((), ())),
        precision=lax.Precision.HIGHEST,
        preferred_element_type=jnp.float32,
    )


def to_windows(field):
    tile_rows, tile_cols, feature = field.shape
    blocks = field.reshape(tile_rows // 16, 16, tile_cols // 16, 16, feature)
    return blocks.transpose(0, 2, 1, 3, 4).reshape(-1, 256, feature)


def from_windows(blocks, tile_rows, tile_cols):
    feature = blocks.shape[-1]
    field = blocks.reshape(tile_rows // 16, tile_cols // 16, 16, 16, feature)
    return field.transpose(0, 2, 1, 3, 4).reshape(tile_rows, tile_cols, feature)


def split_heads(field, heads):
    blocks = to_windows(field)
    count, per_window, feature = blocks.shape
    return blocks.reshape(count, per_window, heads, feature // heads).transpose(2, 0, 1, 3)


def join_heads(stacked, tile_rows, tile_cols):
    heads, count, per_window, depth = stacked.shape
    blocks = stacked.transpose(1, 2, 0, 3).reshape(count, per_window, heads * depth)
    return from_windows(blocks, tile_rows, tile_cols)


def summary_heads(table, heads):
    count, feature = table.shape
    return table.reshape(count, heads, feature // heads).transpose(1, 0, 2)


def join_summary(stacked):
    heads, count, depth = stacked.shape
    return stacked.transpose(1, 0, 2).reshape(count, heads * depth)


def region_allowed(row_flag, col_flag):
    region = row_flag.astype(jnp.int32)[:, None] * 2 + col_flag.astype(jnp.int32)[None, :]
    blocks = to_windows(region[:, :, None])[:, :, 0]
    return blocks[:, :, None] == blocks[:, None, :]


def pool_field(field):
    tile_rows, tile_cols, feature = field.shape
    blocks = field.astype(jnp.float32).reshape(tile_rows // 8, 8, tile_cols // 8, 8, feature)
    return jnp.mean(blocks, axis=(1, 3)).reshape(-1, feature).astype(jnp.bfloat16)


def spread_pool(grad_pooled, tile_rows, tile_cols):
    feature = grad_pooled.shape[-1]
    blocks = grad_pooled.reshape(tile_rows // 8, 1, tile_cols // 8, 1, feature) / 64.0
    blocks = jnp.broadcast_to(blocks, (tile_rows // 8, 8, tile_cols // 8, 8, feature))
    return blocks.reshape(tile_rows, tile_cols, feature)


def one_head(operands, allowed, scale):
    queries, keys_win, values_win, summary_keys, summary_values, grad_attn = operands
    scores_win = jnp.where(allowed, product_of("wid,wjd->wij", queries, keys_win) * scale, NEG_FILL)
    scores_sum = product_of("wid,md->wim", queries, summary_keys) * scale
    highest = jnp.maximum(jnp.max(scores_win, axis=-1), jnp.max(scores_sum, axis=-1))[..., None]
    expo_win = jnp.exp(scores_win - highest)
    expo_sum = jnp.exp(scores_sum - highest)
    denominator = jnp.sum(expo_win, axis=-1, keepdims=True) + jnp.sum(
        expo_sum, axis=-1, keepdims=True
    )
    probs_win = expo_win / denominator
    probs_sum = expo_sum / denominator
    weights_win = probs_win.astype(jnp.bfloat16)
    weights_sum = probs_sum.astype(jnp.bfloat16)
    attended = product_of("wij,wjd->wid", weights_win, values_win) + product_of(
        "wim,md->wid", weights_sum, summary_values
    )
    dprob_win = product_of("wid,wjd->wij", grad_attn, values_win)
    dprob_sum = product_of("wid,md->wim", grad_attn, summary_values)
    inner = jnp.sum(probs_win * dprob_win, axis=-1, keepdims=True) + jnp.sum(
        probs_sum * dprob_sum, axis=-1, keepdims=True
    )
    dscore_win = (probs_win * (dprob_win - inner) * scale).astype(jnp.bfloat16)
    dscore_sum = (probs_sum * (dprob_sum - inner) * scale).astype(jnp.bfloat16)
    grad_q = product_of("wij,wjd->wid", dscore_win, keys_win) + product_of(
        "wim,md->wid", dscore_sum, summary_keys
    )
    grad_k = product_of("wij,wid->wjd", dscore_win, queries)
    grad_v = product_of("wij,wid->wjd", weights_win, grad_attn)
    grad_sk = product_of("wim,wid->md", dscore_sum, queries)
    grad_sv = product_of("wim,wid->md", weights_sum, grad_attn)
    return (
        attended.astype(jnp.bfloat16),
        grad_q.astype(jnp.bfloat16),
        grad_k.astype(jnp.bfloat16),
        grad_v.astype(jnp.bfloat16),
        grad_sk,
        grad_sv,
    )


def attend(queries, keys, values, summary_keys, summary_values, grad_attn, allowed, heads):
    tile_rows, tile_cols, feature = queries.shape
    scale = float(feature // heads) ** (-0.5)
    operands = (
        split_heads(queries, heads),
        split_heads(keys, heads),
        split_heads(values, heads),
        summary_heads(summary_keys, heads),
        summary_heads(summary_values, heads),
        split_heads(grad_attn, heads),
    )
    results = lax.map(lambda stacked: one_head(stacked, allowed, scale), operands)
    attended, grad_q, grad_k, grad_v, grad_sk, grad_sv = results
    return (
        join_heads(attended, tile_rows, tile_cols),
        join_heads(grad_q, tile_rows, tile_cols),
        join_heads(grad_k, tile_rows, tile_cols),
        join_heads(grad_v, tile_rows, tile_cols),
        join_summary(grad_sk),
        join_summary(grad_sv),
    )


def body(features, cotangent, w_query, w_key, w_value, w_out):
    tile_rows, tile_cols, feature = features.shape
    upper = passed_along(features[tile_rows - 8 :], "row", 1)
    stacked = jnp.concatenate([upper, features[: tile_rows - 8]], axis=0)
    leftmost = passed_along(stacked[:, tile_cols - 8 :], "col", 1)
    shifted = jnp.concatenate([leftmost, stacked[:, : tile_cols - 8]], axis=1)
    flat = shifted.reshape(-1, feature)
    queries = project(flat, w_query).reshape(shifted.shape)
    keys = project(flat, w_key).reshape(shifted.shape)
    values = project(flat, w_value).reshape(shifted.shape)
    pooled = pool_field(shifted)
    local_keys = project(pooled, w_key)
    local_values = project(pooled, w_value)
    summary_keys, summary_values = sent_together((local_keys, local_values), ("row", "col"), 0, 1)
    grad_flat = cotangent.reshape(-1, feature)
    grad_attn = times_transposed(grad_flat, w_out).astype(jnp.bfloat16).reshape(shifted.shape)
    row_flag = (jnp.arange(tile_rows) < 8) & (lax.axis_index("row") == 0)
    col_flag = (jnp.arange(tile_cols) < 8) & (lax.axis_index("col") == 0)
    allowed = region_allowed(row_flag, col_flag)
    attended, grad_q, grad_k, grad_v, part_sk, part_sv = attend(
        queries, keys, values, summary_keys, summary_values, grad_attn, allowed, HEADS
    )
    attended_flat = attended.reshape(-1, feature)
    layer_out = (
        (
            flat.astype(jnp.float32)
            + jnp.dot(attended_flat, w_out, preferred_element_type=jnp.float32)
        )
        .astype(jnp.bfloat16)
        .reshape(shifted.shape)
    )
    grad_q = grad_q.reshape(-1, feature)
    grad_k = grad_k.reshape(-1, feature)
    grad_v = grad_v.reshape(-1, feature)
    grad_query = inner_sum(flat, grad_q)
    grad_key = inner_sum(flat, grad_k)
    grad_value = inner_sum(flat, grad_v)
    grad_proj = inner_sum(attended_flat, grad_flat)
    grad_sk, grad_sv = (
        lax.psum_scatter(part_sk, ("row", "col"), scatter_dimension=0, tiled=True),
        lax.psum_scatter(part_sv, ("row", "col"), scatter_dimension=0, tiled=True),
    )
    grad_pooled = transposed_exact(grad_sk, w_key) + transposed_exact(grad_sv, w_value)
    pooled_wide = pooled.astype(jnp.float32)
    grad_key = grad_key + inner_exact(pooled_wide, grad_sk)
    grad_value = grad_value + inner_exact(pooled_wide, grad_sv)
    grad_query, grad_key, grad_value, grad_proj = lax.psum(
        (grad_query, grad_key, grad_value, grad_proj), ("row", "col")
    )
    local_part = (
        times_transposed(grad_q, w_query)
        + times_transposed(grad_k, w_key)
        + times_transposed(grad_v, w_value)
    )
    grad_field = (
        cotangent.astype(jnp.float32)
        + local_part.reshape(shifted.shape)
        + spread_pool(grad_pooled, tile_rows, tile_cols)
    )
    return (layer_out, grad_field.astype(jnp.bfloat16), grad_query, grad_key, grad_value, grad_proj)


def solution(mesh):
    placed = (P("row", "col", None), P("row", "col", None), P(), P(), P(), P())
    return jax.shard_map(
        body,
        mesh=mesh,
        in_specs=placed,
        out_specs=(P("row", "col", None), P("row", "col", None), P(), P(), P(), P()),
        check_vma=False,
    )
```

profile of v0, /device:TPU:1, one launch (start us, length us, event | category | flops | bytes accessed | tf_op | source)
XLA Modules:
  0.0 729.4 jit_solution(13153387075901120608)
XLA Ops:
  8.3 2.5 collective-permute-start
  11.9 6.6 collective-permute-done
  18.6 2.5 collective-permute-start.1
  21.1 4.7 collective-permute-done.1
  30.8 2.3 copy.71
  41.5 2.3 copy.69
  48.1 174.9 %all-gather.3.cloned.1.call-done = bf16[128,12,1024]{2,1,0:T(8,128)(2,1)} async-done(((bf16[1,12,1024]{2,1,0:T(8,128)(2,1)}), bf16[128,12,1024]{2,1,0:T(8,128)(2,1)}) %all-gather.3.cloned.1.call-update) | async-done | bytes 3145744 | tf_op jit(solution)/shard_map/all_gather | solution.py:20
  223.0 6.1 reshape.139
  229.1 3.7 fusion.103
  234.6 2.6 copy.66
  237.2 161.6 %while.21 = (s32[]{:T(128)}, bf16[8,3,256,64]{2,3,1,0:T(8,128)(2,1)}, bf16[8,3,256,64]{2,3,1,0:T(8,128)(2,1)}, bf16[8,3,256,64]{2,3,1,0:T(8,128)(2,1)}, bf16[8,3...) while((s32[]{:T(128)}, ...), condition=%wide.region_8.9_spmd.clone, body=%wide.region_1.8_spmd.clone.sunk | while | flops 1091073792 | bytes 59510444 | solution.py:172
  240.4 1.9 fusion.197
  243.6 2.4 multiply_reduce_fusion.7
  250.8 1.7 fusion.193
  254.6 2.8 fusion.191
  260.6 1.9 fusion.197
  263.8 2.4 multiply_reduce_fusion.7
  271.0 1.7 fusion.193
  274.8 2.8 fusion.191
  280.8 2.0 fusion.197
  284.0 2.4 multiply_reduce_fusion.7
  291.2 1.7 fusion.193
  295.0 2.8 fusion.191
  301.1 2.0 fusion.197
  304.2 2.4 multiply_reduce_fusion.7
  311.4 1.7 fusion.193
  315.2 2.8 fusion.191
  321.3 1.9 fusion.197
  324.5 2.4 multiply_reduce_fusion.7
  335.5 2.8 fusion.191
  341.5 1.9 fusion.197
  344.7 2.4 multiply_reduce_fusion.7
  355.6 2.8 fusion.191
  361.7 1.9 fusion.197
  364.8 2.4 multiply_reduce_fusion.7
  375.8 2.8 fusion.191
  381.9 1.9 fusion.197
  385.0 2.4 multiply_reduce_fusion.7
  396.0 2.8 fusion.191
  402.7 2.1 copy.72
  408.2 147.8 %all-reduce.9.cloned.1.call-done = (f32[1536,512]{0,1:T(8,128)}, f32[1536,512]{0,1:T(8,128)}) async-done(((f32[1536,512]{0,1:T(8,128)}, f32[1536,512]{0,1:T(8,128)}), (f32[1536,512]{0,1:T(8,128)}, f32[1536,512]{0,1:T(8,128)})) %all-reduce.9.cloned.1.call-update) | async-done | bytes 6291472
  557.7 1.7 fusion.92
  562.7 1.9 fusion.104
  567.3 1.8 fusion.94
  569.2 1.9 fusion.86
  572.6 143.6 %all-reduce.7.cloned.1.call-done = (f32[512,512]{1,0:T(8,128)}, f32[512,512]{1,0:T(8,128)}, f32[512,512]{1,0:T(8,128)}, f32[512,512]{1,0:T(8,128)}) async-done(((f32[512,512]{1,0:T(8,128)}, f32[512,512]{1,0:T(8,128)}, f32[512,512]{1,0:T(8,128)}, f32[512,512]{1,0:T(8,128)}), (f32[512,512]{1,0:T(8,128)}, f32[512,512]{1,0:T(8,128)}, f32[512,512]{1,0:T(8,128)}, ...) | async-done | bytes 4194320 | tf_op jit(solution)/shard_map/psum | solution.py:230
  716.2 2.4 copy.123
  718.6 2.3 copy.124
  (244 shorter events, 137.0 us)
Async XLA Ops:
  7.2 19.2 %copy-start = (bf16[512,512]{1,0:T(8,128)(2,1)S(1)}, bf16[512,512]{1,0:T(8,128)(2,1)}, u32[]{:S(2)}) copy-start(bf16[512,512]{1,0:T(8,128)(2,1)} %param.11) | copy-start | bytes 1572868
  7.2 19.0 %copy-start.4 = (bf16[512,512]{1,0:T(8,128)(2,1)S(1)}, bf16[512,512]{1,0:T(8,128)(2,1)}, u32[]{:S(2)}) copy-start(bf16[512,512]{1,0:T(8,128)(2,1)} %param.12) | copy-start | bytes 1572868
  7.2 215.8 %all-gather.3.cloned.1.call-start = ((), (), s32[]{:S(2)}) async-start(), calls=%async_computation | async-start | bytes 4227072 | tf_op jit(solution)/shard_map/all_gather | solution.py:20
  8.2 19.3 %copy-start.6 = (bf16[48,16,512]{2,1,0:T(8,128)(2,1)S(1)}, bf16[48,16,512]{2,1,0:T(8,128)(2,1)}, u32[]{:S(2)}) copy-start(bf16[48,16,512]{2,1,0:T(8,128)(2,1)} %param.9) | copy-start | bytes 2359300
  8.3 10.3 %collective-permute-start = (bf16[8,16,512]{2,1,0:T(8,128)(2,1)S(1)}, bf16[8,16,512]{2,1,0:T(8,128)(2,1)S(1)}, u32[]{:S(2)}, u32[]{:S(2)}) collective-permute-start(bf16[8,16,512]{2,1,0:T(8,128)(2,1)S(1)} %slice.18), channel_id=1, source_target_pairs={{112,0},{0,16},{16,32},{32,48},{48,64},{64,80},{80,96},{96,112},{1... | collective-permute-start | bytes 393224 | tf_op jit(solution)/shard_map/ppermute | solution.py:15
  18.6 7.2 collective-permute-start.1
  25.9 17.9 %copy-start.1 = (bf16[48,16,512]{2,1,0:T(8,128)(2,1)}, bf16[48,16,512]{2,1,0:T(8,128)(2,1)S(1)}, u32[]{:S(2)}) copy-start(bf16[48,16,512]{2,1,0:T(8,128)(2,1)S(1)} %fusion.87) | copy-start | bytes 2359300
  26.2 1.4 copy-start.18
  27.2 528.8 %all-reduce.9.cloned.1.call-start = ((), (), s32[]{:S(2)}) async-start(), calls=%async_computation.2 | async-start | bytes 12582912
  239.3 1.1 copy-start.13
  259.5 1.1 copy-start.13
  279.7 1.1 copy-start.13
  299.9 1.1 copy-start.13
  320.2 1.1 copy-start.13
  340.4 1.1 copy-start.13
  360.5 1.1 copy-start.13
  380.7 1.1 copy-start.13
  398.8 1.1 copy-start.16
  398.8 2.0 copy-start.15
  398.9 317.4 %all-reduce.7.cloned.1.call-start = ((), (), s32[]{:S(2)}) async-start(), calls=%async_computation.1 | async-start | bytes 8388608 | tf_op jit(solution)/shard_map/psum | solution.py:230
  400.6 1.1 copy-start.14
  402.5 2.6 copy-start.2
  402.6 4.0 copy-start.3
  402.7 4.0 copy-start.7
  404.8 151.1 %copy-start.19 = (bf16[12,512]{1,0:T(8,128)(2,1)S(1)}, bf16[12,512]{1,0:T(8,128)(2,1)}, u32[]{:S(2)}) copy-start(bf16[12,512]{1,0:T(8,128)(2,1)} %copy-done.18) | copy-start | bytes 36868
  405.0 1.6 copy-start.9
  561.1 1.6 copy-start.17
  562.7 2.5 copy-start.10
  562.7 2.5 copy-start.20
  564.6 2.1 copy-start.5
  567.3 3.9 copy-start.8
  716.2 4.7 copy-start.12
  716.2 5.7 copy-start.11
Sparse Core Ops, SparseCore 0:
  27.3 195.6 all-gather.2
  399.0 156.9 all-reduce.8
  562.8 153.3 all-reduce.6
where the time goes:
time: 732 us; the launch traced here: 729 us
  waiting for transfers between devices  478 us (65%)
  matrix products  163 us (22%)
  local copies, waits for them, and re-layouts  44.1 us (6%)
  other arithmetic  24.6 us (3%)
  between operations  14.2 us (2%)
    all_gather x1, waiting for transfers between devices, sent_together(): lax.all_gather(both, axis, axis=dim, tiled=True)  175 us
    unnamed x4, waiting for transfers between devices  148 us
    psum x1, waiting for transfers between devices, body(): lax.psum((grad_query, grad_key, grad_value, grad_proj), ('row', 'col'))  144 us
    dot_general x96, matrix products, product_of(): return jnp.einsum(form, left, right, preferred_element_type=jnp.float32)  138 us
    unnamed x53, local copies, waits for them, and re-layouts  21.4 us
  transfers between devices with their start and end apart: 5, of which 5 were waited for; matrix products, arithmetic and copies ran while one was open for 5% of the time, Pallas kernels for 0%

commit v1 on v0

v1 whole, which is shorter than its diff:
```python
import jax, jax.numpy as jnp
from jax import lax
from jax.experimental import pallas as pl
from jax.experimental.pallas import tpu as pltpu
from jax.sharding import PartitionSpec as P

C = 512
NS = 1536
NT = 768
F32, BF16 = jnp.float32, jnp.bfloat16


def dot(a, b):
    return jnp.dot(a, b, preferred_element_type=F32)


def dot_t(a, b):
    return lax.dot_general(a, b, (((1,), (1,)), ((), ())), preferred_element_type=F32)


def main_kernel(x_ref, cot_ref, pool_ref, wq_ref, wk_ref, wv_ref, wo_ref,
                out_ref, base_ref, gp_ref, wg_ref,
                kp, vp, kt, vt, qt, gt, s_scr, we, ds, att_t, gq_t, gk, gv, acc_k, acc_v):
    first_row = lax.axis_index("row") == 0
    first_col = lax.axis_index("col") == 0
    def put_keys(src, first, count):
        for w_ref, dst, dst_t in ((wk_ref, kp, kt), (wv_ref, vp, vt)):
            val = src(w_ref).astype(BF16)
            for p in range(4):
                dst[p, first:first + count, :] = val[:, p * 128:(p + 1) * 128]
            for i in range(count // 256):
                tr = val[i * 256:(i + 1) * 256].T
                for h in range(8):
                    dst_t[h, 0:64, first + i * 256:first + (i + 1) * 256] = tr[h * 64:(h + 1) * 64]
    for i in range(3):
        put_keys(lambda w: dot(pool_ref[0, i * 512:(i + 1) * 512], w[0:256]) + dot(pool_ref[1, i * 512:(i + 1) * 512], w[256:512]),
                 i * 512, 512)
    for w in range(3):
        xw = x_ref[w * 256:(w + 1) * 256]
        put_keys(lambda wr: dot(xw, wr[...]), NS + w * 256, 256)
        qt[w] = (dot(xw, wq_ref[...]).astype(BF16) * jnp.asarray(0.125, BF16)).T
        gt[w] = dot_t(wo_ref[...], cot_ref[w * 256:(w + 1) * 256]).astype(BF16)
    tail = (lax.broadcasted_iota(jnp.int32, (16, 2304), 0) == 0).astype(F32).astype(BF16)
    for h in range(8):
        vt[h, 64:80, :] = tail
    acc_k[...] = jnp.zeros_like(acc_k)
    acc_v[...] = jnp.zeros_like(acc_v)

    def step(it, carry):
        p = it // 3
        w = it % 3
        kwin = pl.ds(pl.multiple_of(NS + w * 256, 256), 256)
        def regions(axis):
            idx = lax.broadcasted_iota(jnp.int32, (256, 256), axis)
            r = jnp.where(((idx // 16) < 8) & first_row & (w == 0), 2, 0)
            return r + jnp.where(((idx % 16) < 8) & first_col, 1, 0)
        def rows_of(ref, c):
            return ref[p, c * 256:(c + 1) * 256, :] if c < 6 else ref[p, kwin, :]
        zeros = jnp.zeros((64, 256), BF16)
        pads = (lambda v: jnp.concatenate([v, zeros], 0), lambda v: jnp.concatenate([zeros, v], 0))
        sides = []
        for hh in range(2):
            h = p * 2 + hh
            hs = pl.ds(pl.multiple_of(h * 64, 64), 64)
            q = qt[w, hs, :]
            g = gt[w, hs, :]
            qm, gm = pads[hh](q), pads[hh](g)
            m8 = None
            for c in range(7):
                s = dot(rows_of(kp, c), qm)
                if c == 6:
                    s = jnp.where(regions(0) == regions(1), s, -1e30)
                s_scr[hh, c * 256:(c + 1) * 256, :] = s
                top = jnp.max(s.reshape(32, 8, 256), axis=0)
                m8 = top if m8 is None else jnp.maximum(m8, top)
            m = jnp.max(m8, axis=0, keepdims=True)
            for c in range(7):
                we[hh, c * 256:(c + 1) * 256, :] = jnp.exp(s_scr[hh, c * 256:(c + 1) * 256, :] - m).astype(BF16)
            a80 = dot(vt[h, :, 0:NS], we[hh, 0:NS, :]) + dot(vt[h, :, kwin], we[hh, NS:, :])
            rinv = 1.0 / a80[64:65, :]
            att = a80[0:64, :] * rinv
            att_t[w, hs, :] = att.astype(BF16)
            inner = jnp.sum(att * g.astype(F32), axis=0, keepdims=True)
            for c in range(7):
                dp = dot(rows_of(vp, c), gm)
                ds[hh, c * 256:(c + 1) * 256, :] = (we[hh, c * 256:(c + 1) * 256, :].astype(F32) * (dp - inner)).astype(BF16)
            dq = dot(kt[h, :, 0:NS], ds[hh, 0:NS, :]) + dot(kt[h, :, kwin], ds[hh, NS:, :])
            gq_t[w, hs, :] = (dq * (rinv * 0.125)).astype(BF16)
            sides.append(((qm.astype(F32) * rinv).astype(BF16), (gm.astype(F32) * rinv).astype(BF16)))
        for c in range(7):
            rows = slice(c * 256, (c + 1) * 256)
            dk = dot_t(ds[0, rows, :], sides[0][0]) + dot_t(ds[1, rows, :], sides[1][0])
            dv = dot_t(we[0, rows, :], sides[0][1]) + dot_t(we[1, rows, :], sides[1][1])
            if c < 6:
                acc_k[p, rows, :] += dk
                acc_v[p, rows, :] += dv
            else:
                gk[w, p] = dk.astype(BF16)
                gv[w, p] = dv.astype(BF16)
        return carry

    lax.fori_loop(0, 12, step, 0)

    wg_acc = [None] * 4
    for w in range(3):
        rows = slice(w * 256, (w + 1) * 256)
        xw = x_ref[rows]
        cw = cot_ref[rows]
        a_t = att_t[w]
        out_ref[rows] = (xw.astype(F32) + dot(a_t.T, wo_ref[...])).astype(BF16)
        gqw = gq_t[w].T
        gkw = jnp.concatenate([gk[w, p] for p in range(4)], 1)
        gvw = jnp.concatenate([gv[w, p] for p in range(4)], 1)
        base_ref[rows] = cw.astype(F32) + dot_t(gqw, wq_ref[...]) + dot_t(gkw, wk_ref[...]) + dot_t(gvw, wv_ref[...])
        xt = xw.T
        for i, (a, b) in enumerate(((xt, gqw), (xt, gkw), (xt, gvw), (a_t, cw))):
            t = dot(a, b)
            wg_acc[i] = t if w == 0 else wg_acc[i] + t
    sk = jnp.concatenate([acc_k[p].astype(BF16) for p in range(4)], 1)
    sv = jnp.concatenate([acc_v[p].astype(BF16) for p in range(4)], 1)
    for i in range(3):
        rows = slice(i * 512, (i + 1) * 512)
        gp_ref[rows] = (dot_t(sk[rows], wk_ref[...]) + dot_t(sv[rows], wv_ref[...])).astype(BF16)
        pt = jnp.concatenate([pool_ref[0, rows].T, pool_ref[1, rows].T], 0)
        wg_acc[1] += dot(pt, sk[rows])
        wg_acc[2] += dot(pt, sv[rows])
    for i in range(4):
        wg_ref[i * 512:(i + 1) * 512] = wg_acc[i].astype(BF16)


def main_call(x, cot, pool, wq, wk, wv, wo):
    vm = pl.BlockSpec(memory_space=pltpu.VMEM)
    return pl.pallas_call(
        main_kernel,
        out_shape=(jax.ShapeDtypeStruct((NT, C), BF16), jax.ShapeDtypeStruct((NT, C), F32),
                   jax.ShapeDtypeStruct((NS, C), BF16), jax.ShapeDtypeStruct((2048, C), BF16)),
        in_specs=[vm] * 7, out_specs=(vm,) * 4,
        scratch_shapes=[
            pltpu.VMEM((4, 2304, 128), BF16), pltpu.VMEM((4, 2304, 128), BF16),
            pltpu.VMEM((8, 64, 2304), BF16), pltpu.VMEM((8, 80, 2304), BF16),
            pltpu.VMEM((3, 512, 256), BF16), pltpu.VMEM((3, 512, 256), BF16),
            pltpu.VMEM((2, 1792, 256), F32), pltpu.VMEM((2, 1792, 256), BF16), pltpu.VMEM((2, 1792, 256), BF16),
            pltpu.VMEM((3, 512, 256), BF16), pltpu.VMEM((3, 512, 256), BF16),
            pltpu.VMEM((3, 4, 256, 128), BF16), pltpu.VMEM((3, 4, 256, 128), BF16),
            pltpu.VMEM((4, NS, 128), F32), pltpu.VMEM((4, NS, 128), F32),
        ],
        compiler_params=pltpu.CompilerParams(vmem_limit_bytes=60 * 1024 * 1024),
        name="attention",
    )(x, cot, pool, wq, wk, wv, wo)


ROWS, COLS, CHIPS = 8, 16, 64
MESH_ID = pl.DeviceIdType.MESH


def place():
    row, col = lax.axis_index("row"), lax.axis_index("col")
    core = lax.rem(col, 2)
    return row, col, core, row * 8 + lax.div(col, 2)


def chip_device(chip, core):
    return (lax.div(chip, 8), lax.rem(chip, 8) * 2 + core)


def neighbour(row, col, down, right):
    return (lax.rem(row + down + ROWS, ROWS), lax.rem(col + right + COLS, COLS))


def meet(row, col, core, chip):
    barrier = pltpu.get_barrier_semaphore()

    def greet(i, carry):
        pl.semaphore_signal(barrier, inc=1, device_id=chip_device(lax.rem(chip + i, CHIPS), core), device_id_type=MESH_ID)
        return carry

    lax.fori_loop(1, CHIPS, greet, 0)
    for down, right in ((0, 1), (1, 1), (0, -1), (-1, -1)):
        pl.semaphore_signal(barrier, inc=1, device_id=neighbour(row, col, down, right), device_id_type=MESH_ID)
    return barrier


def remote(src, dst, send, recv, device):
    return pltpu.make_async_remote_copy(src_ref=src, dst_ref=dst, send_sem=send, recv_sem=recv,
                                        device_id=device, device_id_type=MESH_ID)


def to_all_chips(src_of, dst, send, recv, chip, core):
    def one(i, carry):
        peer = lax.rem(chip + i, CHIPS)
        remote(src_of(peer), dst, send, recv, chip_device(peer, core)).start()
        return carry

    lax.fori_loop(1, CHIPS, one, 0)


def drain(buf, sem):
    pltpu.make_async_copy(buf, buf, sem).wait()


def gather_kernel(f_ref, shifted_ref, pool_ref, mean, other, mine, sem_s, sem_r):
    row, col, core, chip = place()
    partner = (row, col + 1 - 2 * core)
    barrier = meet(row, col, core, chip)
    for i in range(6):
        total = jnp.sum(f_ref[8 * i:8 * i + 8].astype(F32), axis=0)
        mean[2 * i:2 * i + 2, :] = jnp.sum(total.reshape(2, 8, C), axis=1) * (1.0 / 64.0)
    mean[12:16, :] = jnp.zeros((4, C), F32)
    pl.semaphore_wait(barrier, CHIPS - 1 + 4)
    swap = remote(mean.at[:, pl.ds(pl.multiple_of((1 - core) * 256, 256), 256)], other, sem_s.at[0], sem_r.at[0], partner)
    swap.start()
    halo = [
        remote(f_ref.at[0:40, 8:16], shifted_ref.at[8:48, 0:8], sem_s.at[1], sem_r.at[1], neighbour(row, col, 0, 1)),
        remote(f_ref.at[40:48, 0:8], shifted_ref.at[0:8, 8:16], sem_s.at[2], sem_r.at[2], neighbour(row, col, 1, 0)),
        remote(f_ref.at[40:48, 8:16], shifted_ref.at[0:8, 0:8], sem_s.at[3], sem_r.at[3], neighbour(row, col, 1, 1)),
    ]
    swap.wait()
    own = mean[:, pl.ds(pl.multiple_of(core * 256, 256), 256)]
    got = other[...]
    first = jnp.where(core == 0, own, got)
    second = jnp.where(core == 0, got, own)
    mine[...] = jnp.concatenate([first[0:12], second[0:12]], 0).astype(BF16)
    to_all_chips(lambda peer: mine, pool_ref.at[core, chip], sem_s.at[4], sem_r.at[4], chip, core)
    for copy in halo:
        copy.start()
    keep = pltpu.make_async_copy(mine, pool_ref.at[core, chip], sem_s.at[6])
    keep.start()
    shifted_ref[8:48, 8:16, :] = f_ref[0:40, 0:8, :]
    keep.wait()
    drain(pool_ref.at[core, 0:CHIPS - 1], sem_r.at[4])
    last = remote(pool_ref.at[core], pool_ref.at[core], sem_s.at[5], sem_r.at[5], partner)
    last.start()
    for copy in halo:
        copy.wait()
    drain(pool_ref.at[core, 0:CHIPS - 1], sem_s.at[4])
    last.wait()


def gather_call(features):
    vm = pl.BlockSpec(memory_space=pltpu.VMEM)
    return pl.pallas_call(
        gather_kernel,
        out_shape=(jax.ShapeDtypeStruct((48, 16, C), BF16), jax.ShapeDtypeStruct((2, CHIPS, 24, 256), BF16)),
        in_specs=[vm], out_specs=(vm, vm),
        scratch_shapes=[pltpu.VMEM((16, C), F32), pltpu.VMEM((16, 256), F32), pltpu.VMEM((24, 256), BF16),
                        pltpu.SemaphoreType.DMA((7,)), pltpu.SemaphoreType.DMA((6,))],
        compiler_params=pltpu.CompilerParams(collective_id=0, has_side_effects=True),
        name="gather",
    )(features)


def reduce_kernel(gp_ref, wg_ref, pooled_ref, weights_ref,
                  gp_in, wg_in, gp_s, wg_s, gp_r, wg_r, half, half_in, block, block_in, mine, sem_s, sem_r):
    row, col, core, chip = place()
    partner = (row, col + 1 - 2 * core)
    barrier = meet(row, col, core, chip)
    pl.semaphore_wait(barrier, CHIPS - 1 + 4)
    theirs = pl.ds(pl.multiple_of((1 - core) * 256, 256), 256)
    ours = pl.ds(pl.multiple_of(core * 256, 256), 256)
    swap_w = remote(wg_ref.at[:, :, theirs], wg_in, sem_s.at[0], sem_r.at[0], partner)
    swap_g = remote(gp_ref.at[:, :, theirs], gp_in, sem_s.at[1], sem_r.at[1], partner)
    swap_w.start()
    swap_g.start()

    def add_up(a, b, dst):
        def one(i, carry):
            dst[i] = (a[i, :, ours].astype(F32) + b[i].astype(F32)).astype(BF16)
            return carry
        lax.fori_loop(0, CHIPS, one, 0)

    def total(buf, rows):
        def one(i, carry):
            return carry + buf[i].astype(F32)
        return lax.fori_loop(0, CHIPS, one, jnp.zeros((rows, 256), F32))

    swap_w.wait()
    add_up(wg_ref, wg_in, wg_s)
    to_all_chips(lambda peer: wg_s.at[peer], wg_r.at[chip], sem_s.at[2], sem_r.at[2], chip, core)
    swap_g.wait()
    add_up(gp_ref, gp_in, gp_s)
    to_all_chips(lambda peer: gp_s.at[peer], gp_r.at[chip], sem_s.at[3], sem_r.at[3], chip, core)
    wg_r[chip] = wg_s[chip]
    gp_r[chip] = gp_s[chip]
    drain(wg_r.at[0:CHIPS - 1], sem_r.at[2])
    mine[...] = total(wg_r, 32).astype(BF16)
    to_all_chips(lambda peer: mine, weights_ref.at[core, chip], sem_s.at[4], sem_r.at[4], chip, core)
    keep = pltpu.make_async_copy(mine, weights_ref.at[core, chip], sem_s.at[7])
    keep.start()
    drain(gp_r.at[0:CHIPS - 1], sem_r.at[3])
    half[...] = total(gp_r, 24)
    swap_h = remote(half, half_in, sem_s.at[5], sem_r.at[5], partner)
    swap_h.start()
    swap_h.wait()
    own, got = half[...], half_in[...]
    both = jnp.concatenate([jnp.where(core == 0, own, got), jnp.where(core == 0, got, own)], 1)
    block[0:12, :] = jnp.where(core == 0, both[0:12], both[12:24])
    block[12:16, :] = jnp.zeros((4, C), F32)
    spread = [remote(block, block_in.at[k], sem_s.at[8 + k], sem_r.at[6 + k], neighbour(row, col, *way))
              for k, way in enumerate(((0, 1), (1, 0), (1, 1)))]
    for copy in spread:
        copy.start()
    for copy in spread:
        copy.wait()
    for i in range(6):
        for j in range(2):
            src = (5 if i == 0 else i - 1) * 2 + 1 - j
            if i == 0:
                val = block_in[2, src:src + 1, :] if j == 0 else block_in[1, src:src + 1, :]
            else:
                val = block_in[0, src:src + 1, :] if j == 0 else block[src:src + 1, :]
            pooled_ref[2 * i + j:2 * i + j + 1, :] = val
    keep.wait()
    drain(weights_ref.at[core, 0:CHIPS - 1], sem_r.at[4])
    last = remote(weights_ref.at[core], weights_ref.at[core], sem_s.at[6], sem_r.at[9], partner)
    last.start()
    drain(wg_r.at[0:CHIPS - 1], sem_s.at[2])
    drain(gp_r.at[0:CHIPS - 1], sem_s.at[3])
    drain(weights_ref.at[core, 0:CHIPS - 1], sem_s.at[4])
    last.wait()


def reduce_call(gp, wg):
    vm = pl.BlockSpec(memory_space=pltpu.VMEM)
    return pl.pallas_call(
        reduce_kernel,
        out_shape=(jax.ShapeDtypeStruct((12, C), F32), jax.ShapeDtypeStruct((2, CHIPS, 32, 256), BF16)),
        in_specs=[vm, vm], out_specs=(vm, vm),
        scratch_shapes=[
            pltpu.VMEM((CHIPS, 24, 256), BF16), pltpu.VMEM((CHIPS, 32, 256), BF16),
            pltpu.VMEM((CHIPS, 24, 256), BF16), pltpu.VMEM((CHIPS, 32, 256), BF16),
            pltpu.VMEM((CHIPS, 24, 256), BF16), pltpu.VMEM((CHIPS, 32, 256), BF16),
            pltpu.VMEM((24, 256), F32), pltpu.VMEM((24, 256), F32),
            pltpu.VMEM((16, C), F32), pltpu.VMEM((3, 16, C), F32), pltpu.VMEM((32, 256), BF16),
            pltpu.SemaphoreType.DMA((11,)), pltpu.SemaphoreType.DMA((10,)),
        ],
        compiler_params=pltpu.CompilerParams(collective_id=1, has_side_effects=True),
        name="reduce",
    )(gp.reshape(CHIPS, 24, C), wg.reshape(CHIPS, 32, C))


def body(features, cotangent, w_query, w_key, w_value, w_out):
    shifted, pool = gather_call(features)
    out, base, gp, wg = main_call(shifted.reshape(NT, C), cotangent.reshape(NT, C), pool.reshape(2, NS, 256),
                                  w_query, w_key, w_value, w_out)
    pooled, weights = reduce_call(gp, wg)
    share = jnp.broadcast_to((pooled * (1.0 / 64.0)).reshape(6, 1, 2, 1, C), (6, 8, 2, 8, C)).reshape(48, 16, C)
    grad_features = (base.reshape(48, 16, C) + share).astype(BF16)
    grads = weights.reshape(2, 4, C, 256).transpose(1, 2, 0, 3).reshape(4, C, C).astype(F32)
    return (out.reshape(48, 16, C), grad_features, grads[0], grads[1], grads[2], grads[3])


def solution(mesh):
    tile = P("row", "col", None)
    return jax.shard_map(body, mesh=mesh, in_specs=(tile, tile, P(), P(), P(), P()),
                         out_specs=(tile, tile, P(), P(), P(), P()), check_vma=False)
```

time: 732 us -> 165 us (0.23)
  waiting for transfers between devices: 478 us -> 0 us
  matrix products: 163 us -> 0 us
  Pallas kernels: 0 us -> 151 us
  local copies, waits for them, and re-layouts: 44.1 us -> 8.93 us
  other arithmetic: 24.6 us -> 2.41 us
  between operations: 14.2 us -> 0.7 us
    all_gather x1 -> x0, waiting for transfers between devices: 175 us -> none  [sent_together(): lax.all_gather(both, axis, axis=dim, tiled=True)]
    dot_general x114 -> x0, matrix products: 163 us -> none  [the longest x96 138 us: product_of(): return jnp.einsum(form, left, right, preferred_element_type=jnp.float32)]
    pallas_call x0 -> x3, Pallas kernels: none -> 151 us  [the longest x1 61.9 us: main_call(): pl.pallas_call(main_kernel, out_shape=(jax.ShapeDtypeStruct((NT, C), BF16...]
    unnamed x4 -> x0, waiting for transfers between devices: 148 us -> none
    psum x1 -> x0, waiting for transfers between devices: 144 us -> none  [body(): lax.psum((grad_query, grad_key, grad_value, grad_proj), ('row', 'col'))]
    unnamed x53 -> x8, local copies, waits for them, and re-layouts: 21.4 us -> 5.2 us
    convert_element_type x19 -> x2, other arithmetic: 15.3 us -> 1.53 us  [the longest x1 1.15 us: body(): grad_features = (base.reshape(48, 16, C) + share).astype(BF16)]
    ppermute x2 -> x0, waiting for transfers between devices: 11.4 us -> none  [passed_along(): return lax.ppermute(block, axis, route)]
  transfers between devices with their start and end apart: 5 -> 0, of which waited for: 5 -> 0; matrix products, arithmetic and copies ran while one was open for 5% -> 0% of each run, Pallas kernels for 0% -> 0%
where the time goes in v1:
time: 165 us; the launch traced here: 163 us
  Pallas kernels  151 us (92%)
  local copies, waits for them, and re-layouts  8.93 us (5%)
  other arithmetic  2.41 us (1%)
    pallas_call x1, Pallas kernels, main_call(): pl.pallas_call(main_kernel, out_shape=(jax.ShapeDtypeStruct((NT, C), BF16...  61.9 us
    pallas_call x1, Pallas kernels, reduce_call(): pl.pallas_call(reduce_kernel, out_shape=(jax.ShapeDtypeStruct((12, C), F3...  59.2 us
    pallas_call x1, Pallas kernels, gather_call(): pl.pallas_call(gather_kernel, out_shape=(jax.ShapeDtypeStruct((48, 16, C)...  29.7 us
    unnamed x8, local copies, waits for them, and re-layouts  5.2 us

profile of v1, /device:TPU:1, one launch (start us, length us, event | category | flops | bytes accessed | tf_op | source)
XLA Modules:
  0.0 162.9 jit_solution(15457404998390885943)
XLA Ops:
  0.6 29.7 %gather.1 = (bf16[48,16,512]{2,1,0:T(8,128)(2,1)}, bf16[2,64,24,256]{3,2,1,0:T(8,128)(2,1)}) custom-call(bf16[48,16,512]{2,1,0:T(8,128)(2,1)} %f_ref.1), custom_call_target="tpu_custom_call" | custom-call | tf_op jit(solution)/shard_map/gather/pallas_call | solution.py:241
  30.3 61.9 %attention.1 = (bf16[768,512]{1,0:T(8,128)(2,1)}, f32[768,512]{1,0:T(8,128)}, bf16[1536,512]{1,0:T(8,128)(2,1)}, bf16[2048,512]{1,0:T(8,128)(2,1)}) custom-call(bf16[768,512]{1,0:T(8,128)(2,1)} %bitcast.41, bf16[768,512]{1,0:T(8,128)(2,1)} %bitcast.40, bf16[2,1536,256]{2,1,0:T(8,128)(2,1)} %bitcast.35, bf16[512,512]{1,0:T(8,128)(2,1)} %wq_ref.1, ...), custom_call_target="tpu_custom_call" | custom-call | tf_op jit(solution)/shard_map/attention/pallas_call | solution.py:133
  92.2 59.2 %reduce.1 = (f32[12,512]{1,0:T(8,128)}, bf16[2,64,32,256]{3,2,1,0:T(8,128)(2,1)}) custom-call(bf16[64,24,512]{2,1,0:T(8,128)(2,1)} %bitcast.33, bf16[64,32,512]{2,1,0:T(8,128)(2,1)} %bitcast.32), custom_call_target="tpu_custom_call" | custom-call | tf_op jit(solution)/shard_map/reduce/pallas_call | solution.py:324
  151.5 0.0 copy-start.1
  151.5 0.9 broadcast_multiply_fusion
  152.4 0.2 broadcast_in_dim.8
  152.6 0.3 copy-done.1
  152.9 0.0 copy-start
  152.9 1.2 add_convert_fusion
  154.0 0.7 copy-done
  154.8 0.4 convert_bitcast_fusion
  155.1 0.3 fusion
  155.4 0.8 copy.15
  156.3 1.0 copy.19
  157.3 0.8 copy.14
  158.1 1.0 copy.18
  159.2 0.8 copy.13
  160.0 1.0 copy.17
  161.0 0.8 copy.12
  161.8 1.0 copy.16
  (1 shorter events, 0.0 us)
Async XLA Ops:
  151.5 1.4 copy-start.1
  152.9 1.9 %copy-start = (bf16[2,64,32,256]{3,2,1,0:T(8,128)(2,1)S(1)}, bf16[2,64,32,256]{3,2,1,0:T(8,128)(2,1)}, u32[]{:S(2)}) copy-start(bf16[2,64,32,256]{3,2,1,0:T(8,128)(2,1)} %get-tuple-element.21) | copy-start | bytes 6291460

commit v2 on v1

--- a/solution.py
+++ b/solution.py
@@ -18,25 +18,26 @@
     return lax.dot_general(a, b, (((1,), (1,)), ((), ())), preferred_element_type=F32)
 
 
-def main_kernel(x_ref, cot_ref, pool_ref, wq_ref, wk_ref, wv_ref, wo_ref,
+def main_kernel(f_ref, cot_ref, wq_ref, wk_ref, wv_ref, wo_ref,
                 out_ref, base_ref, gp_ref, wg_ref,
-                kp, vp, kt, vt, qt, gt, s_scr, we, ds, att_t, gq_t, gk, gv, acc_k, acc_v):
+                x_ref, pool_ref, mean, other, mine, sem_s, sem_r, kp, vp, kt, vt, qt, gt, s_scr, we, ds, att_t, gq_t, gk, gv, acc_k, acc_v):
     first_row = lax.axis_index("row") == 0
     first_col = lax.axis_index("col") == 0
+    halo, finish_gather = start_gather(f_ref, x_ref, pool_ref, mean, other, mine, sem_s, sem_r)
+
     def put_keys(src, first, count):
         for w_ref, dst, dst_t in ((wk_ref, kp, kt), (wv_ref, vp, vt)):
             val = src(w_ref).astype(BF16)
             for p in range(4):
                 dst[p, first:first + count, :] = val[:, p * 128:(p + 1) * 128]
-            for i in range(count // 256):
-                tr = val[i * 256:(i + 1) * 256].T
+            for i in range(count // 128):
+                tr = val[i * 128:(i + 1) * 128].T
                 for h in range(8):
-                    dst_t[h, 0:64, first + i * 256:first + (i + 1) * 256] = tr[h * 64:(h + 1) * 64]
-    for i in range(3):
-        put_keys(lambda w: dot(pool_ref[0, i * 512:(i + 1) * 512], w[0:256]) + dot(pool_ref[1, i * 512:(i + 1) * 512], w[256:512]),
-                 i * 512, 512)
+                    dst_t[h, 0:64, first + i * 128:first + (i + 1) * 128] = tr[h * 64:(h + 1) * 64]
+    for copy in halo:
+        copy.wait()
     for w in range(3):
-        xw = x_ref[w * 256:(w + 1) * 256]
+        xw = x_ref[w * 16:(w + 1) * 16].reshape(256, C)
         put_keys(lambda wr: dot(xw, wr[...]), NS + w * 256, 256)
         qt[w] = (dot(xw, wq_ref[...]).astype(BF16) * jnp.asarray(0.125, BF16)).T
         gt[w] = dot_t(wo_ref[...], cot_ref[w * 256:(w + 1) * 256]).astype(BF16)
@@ -45,6 +46,14 @@
         vt[h, 64:80, :] = tail
     acc_k[...] = jnp.zeros_like(acc_k)
     acc_v[...] = jnp.zeros_like(acc_v)
+    finish_gather()
+
+    def pool_rows(half, i):
+        return pool_ref[half, i * 16:(i + 1) * 16].reshape(384, 256)
+
+    for i in range(4):
+        put_keys(lambda w: dot(pool_rows(0, i), w[0:256]) + dot(pool_rows(1, i), w[256:512]),
+                 i * 384, 384)
 
     def step(it, carry):
         p = it // 3
@@ -104,7 +113,7 @@
     wg_acc = [None] * 4
     for w in range(3):
         rows = slice(w * 256, (w + 1) * 256)
-        xw = x_ref[rows]
+        xw = x_ref[w * 16:(w + 1) * 16].reshape(256, C)
         cw = cot_ref[rows]
         a_t = att_t[w]
         out_ref[rows] = (xw.astype(F32) + dot(a_t.T, wo_ref[...])).astype(BF16)
@@ -118,24 +127,27 @@
             wg_acc[i] = t if w == 0 else wg_acc[i] + t
     sk = jnp.concatenate([acc_k[p].astype(BF16) for p in range(4)], 1)
     sv = jnp.concatenate([acc_v[p].astype(BF16) for p in range(4)], 1)
-    for i in range(3):
-        rows = slice(i * 512, (i + 1) * 512)
+    for i in range(4):
+        rows = slice(i * 384, (i + 1) * 384)
         gp_ref[rows] = (dot_t(sk[rows], wk_ref[...]) + dot_t(sv[rows], wv_ref[...])).astype(BF16)
-        pt = jnp.concatenate([pool_ref[0, rows].T, pool_ref[1, rows].T], 0)
+        pt = jnp.concatenate([pool_rows(0, i).T, pool_rows(1, i).T], 0)
         wg_acc[1] += dot(pt, sk[rows])
         wg_acc[2] += dot(pt, sv[rows])
     for i in range(4):
         wg_ref[i * 512:(i + 1) * 512] = wg_acc[i].astype(BF16)
 
 
-def main_call(x, cot, pool, wq, wk, wv, wo):
+def main_call(features, cot, wq, wk, wv, wo):
     vm = pl.BlockSpec(memory_space=pltpu.VMEM)
     return pl.pallas_call(
         main_kernel,
         out_shape=(jax.ShapeDtypeStruct((NT, C), BF16), jax.ShapeDtypeStruct((NT, C), F32),
                    jax.ShapeDtypeStruct((NS, C), BF16), jax.ShapeDtypeStruct((2048, C), BF16)),
-        in_specs=[vm] * 7, out_specs=(vm,) * 4,
+        in_specs=[vm] * 6, out_specs=(vm,) * 4,
         scratch_shapes=[
+            pltpu.VMEM((48, 16, C), BF16), pltpu.VMEM((2, CHIPS, 24, 256), BF16),
+            pltpu.VMEM((16, C), F32), pltpu.VMEM((16, 256), F32), pltpu.VMEM((24, 256), BF16),
+            pltpu.SemaphoreType.DMA((7,)), pltpu.SemaphoreType.DMA((6,)),
             pltpu.VMEM((4, 2304, 128), BF16), pltpu.VMEM((4, 2304, 128), BF16),
             pltpu.VMEM((8, 64, 2304), BF16), pltpu.VMEM((8, 80, 2304), BF16),
             pltpu.VMEM((3, 512, 256), BF16), pltpu.VMEM((3, 512, 256), BF16),
@@ -144,9 +156,9 @@
             pltpu.VMEM((3, 4, 256, 128), BF16), pltpu.VMEM((3, 4, 256, 128), BF16),
             pltpu.VMEM((4, NS, 128), F32), pltpu.VMEM((4, NS, 128), F32),
         ],
-        compiler_params=pltpu.CompilerParams(vmem_limit_bytes=60 * 1024 * 1024),
+        compiler_params=pltpu.CompilerParams(vmem_limit_bytes=60 * 1024 * 1024, collective_id=0, has_side_effects=True),
         name="attention",
-    )(x, cot, pool, wq, wk, wv, wo)
+    )(features, cot, wq, wk, wv, wo)
 
 
 ROWS, COLS, CHIPS = 8, 16, 64
@@ -198,7 +210,7 @@
     pltpu.make_async_copy(buf, buf, sem).wait()
 
 
-def gather_kernel(f_ref, shifted_ref, pool_ref, mean, other, mine, sem_s, sem_r):
+def start_gather(f_ref, shifted_ref, pool_ref, mean, other, mine, sem_s, sem_r):
     row, col, core, chip = place()
     partner = (row, col + 1 - 2 * core)
     barrier = meet(row, col, core, chip)
@@ -226,27 +238,16 @@
     keep = pltpu.make_async_copy(mine, pool_ref.at[core, chip], sem_s.at[6])
     keep.start()
     shifted_ref[8:48, 8:16, :] = f_ref[0:40, 0:8, :]
-    keep.wait()
-    drain(pool_ref.at[core, 0:CHIPS - 1], sem_r.at[4])
-    last = remote(pool_ref.at[core], pool_ref.at[core], sem_s.at[5], sem_r.at[5], partner)
-    last.start()
-    for copy in halo:
-        copy.wait()
-    drain(pool_ref.at[core, 0:CHIPS - 1], sem_s.at[4])
-    last.wait()
-
-
-def gather_call(features):
-    vm = pl.BlockSpec(memory_space=pltpu.VMEM)
-    return pl.pallas_call(
-        gather_kernel,
-        out_shape=(jax.ShapeDtypeStruct((48, 16, C), BF16), jax.ShapeDtypeStruct((2, CHIPS, 24, 256), BF16)),
-        in_specs=[vm], out_specs=(vm, vm),
-        scratch_shapes=[pltpu.VMEM((16, C), F32), pltpu.VMEM((16, 256), F32), pltpu.VMEM((24, 256), BF16),
-                        pltpu.SemaphoreType.DMA((7,)), pltpu.SemaphoreType.DMA((6,))],
-        compiler_params=pltpu.CompilerParams(collective_id=0, has_side_effects=True),
-        name="gather",
-    )(features)
+
+    def finish():
+        keep.wait()
+        drain(pool_ref.at[core, 0:CHIPS - 1], sem_r.at[4])
+        last = remote(pool_ref.at[core], pool_ref.at[core], sem_s.at[5], sem_r.at[5], partner)
+        last.start()
+        drain(pool_ref.at[core, 0:CHIPS - 1], sem_s.at[4])
+        last.wait()
+
+    return halo, finish
 
 
 def reduce_kernel(gp_ref, wg_ref, pooled_ref, weights_ref,
@@ -257,37 +258,37 @@
     pl.semaphore_wait(barrier, CHIPS - 1 + 4)
     theirs = pl.ds(pl.multiple_of((1 - core) * 256, 256), 256)
     ours = pl.ds(pl.multiple_of(core * 256, 256), 256)
-    swap_w = remote(wg_ref.at[:, :, theirs], wg_in, sem_s.at[0], sem_r.at[0], partner)
+    swap_w = remote(wg_ref.at[1 - core], wg_in, sem_s.at[0], sem_r.at[0], partner)
     swap_g = remote(gp_ref.at[:, :, theirs], gp_in, sem_s.at[1], sem_r.at[1], partner)
     swap_w.start()
     swap_g.start()
 
     def add_up(a, b, dst):
         def one(i, carry):
-            dst[i] = (a[i, :, ours].astype(F32) + b[i].astype(F32)).astype(BF16)
+            dst[i] = (a(i).astype(F32) + b[i].astype(F32)).astype(BF16)
             return carry
         lax.fori_loop(0, CHIPS, one, 0)
 
-    def total(buf, rows):
+    def total(buf, rows, lanes):
         def one(i, carry):
             return carry + buf[i].astype(F32)
-        return lax.fori_loop(0, CHIPS, one, jnp.zeros((rows, 256), F32))
+        return lax.fori_loop(0, CHIPS, one, jnp.zeros((rows, lanes), F32))
 
     swap_w.wait()
-    add_up(wg_ref, wg_in, wg_s)
+    add_up(lambda i: wg_ref[core, i], wg_in, wg_s)
     to_all_chips(lambda peer: wg_s.at[peer], wg_r.at[chip], sem_s.at[2], sem_r.at[2], chip, core)
     swap_g.wait()
-    add_up(gp_ref, gp_in, gp_s)
+    add_up(lambda i: gp_ref[i, :, ours], gp_in, gp_s)
     to_all_chips(lambda peer: gp_s.at[peer], gp_r.at[chip], sem_s.at[3], sem_r.at[3], chip, core)
     wg_r[chip] = wg_s[chip]
     gp_r[chip] = gp_s[chip]
     drain(wg_r.at[0:CHIPS - 1], sem_r.at[2])
-    mine[...] = total(wg_r, 32).astype(BF16)
+    mine[...] = total(wg_r, 16, C).astype(BF16)
     to_all_chips(lambda peer: mine, weights_ref.at[core, chip], sem_s.at[4], sem_r.at[4], chip, core)
     keep = pltpu.make_async_copy(mine, weights_ref.at[core, chip], sem_s.at[7])
     keep.start()
     drain(gp_r.at[0:CHIPS - 1], sem_r.at[3])
-    half[...] = total(gp_r, 24)
+    half[...] = total(gp_r, 24, 256)
     swap_h = remote(half, half_in, sem_s.at[5], sem_r.at[5], partner)
     swap_h.start()
     swap_h.wait()
@@ -323,29 +324,27 @@
     vm = pl.BlockSpec(memory_space=pltpu.VMEM)
     return pl.pallas_call(
         reduce_kernel,
-        out_shape=(jax.ShapeDtypeStruct((12, C), F32), jax.ShapeDtypeStruct((2, CHIPS, 32, 256), BF16)),
+        out_shape=(jax.ShapeDtypeStruct((12, C), F32), jax.ShapeDtypeStruct((2, CHIPS, 16, C), BF16)),
         in_specs=[vm, vm], out_specs=(vm, vm),
         scratch_shapes=[
-            pltpu.VMEM((CHIPS, 24, 256), BF16), pltpu.VMEM((CHIPS, 32, 256), BF16),
-            pltpu.VMEM((CHIPS, 24, 256), BF16), pltpu.VMEM((CHIPS, 32, 256), BF16),
-            pltpu.VMEM((CHIPS, 24, 256), BF16), pltpu.VMEM((CHIPS, 32, 256), BF16),
+            pltpu.VMEM((CHIPS, 24, 256), BF16), pltpu.VMEM((CHIPS, 16, C), BF16),
+            pltpu.VMEM((CHIPS, 24, 256), BF16), pltpu.VMEM((CHIPS, 16, C), BF16),
+            pltpu.VMEM((CHIPS, 24, 256), BF16), pltpu.VMEM((CHIPS, 16, C), BF16),
             pltpu.VMEM((24, 256), F32), pltpu.VMEM((24, 256), F32),
-            pltpu.VMEM((16, C), F32), pltpu.VMEM((3, 16, C), F32), pltpu.VMEM((32, 256), BF16),
+            pltpu.VMEM((16, C), F32), pltpu.VMEM((3, 16, C), F32), pltpu.VMEM((16, C), BF16),
             pltpu.SemaphoreType.DMA((11,)), pltpu.SemaphoreType.DMA((10,)),
         ],
         compiler_params=pltpu.CompilerParams(collective_id=1, has_side_effects=True),
         name="reduce",
-    )(gp.reshape(CHIPS, 24, C), wg.reshape(CHIPS, 32, C))
+    )(gp.reshape(CHIPS, 24, C), wg.reshape(2, CHIPS, 16, C))
 
 
 def body(features, cotangent, w_query, w_key, w_value, w_out):
-    shifted, pool = gather_call(features)
-    out, base, gp, wg = main_call(shifted.reshape(NT, C), cotangent.reshape(NT, C), pool.reshape(2, NS, 256),
-                                  w_query, w_key, w_value, w_out)
+    out, base, gp, wg = main_call(features, cotangent.reshape(NT, C), w_query, w_key, w_value, w_out)
     pooled, weights = reduce_call(gp, wg)
     share = jnp.broadcast_to((pooled * (1.0 / 64.0)).reshape(6, 1, 2, 1, C), (6, 8, 2, 8, C)).reshape(48, 16, C)
     grad_features = (base.reshape(48, 16, C) + share).astype(BF16)
-    grads = weights.reshape(2, 4, C, 256).transpose(1, 2, 0, 3).reshape(4, C, C).astype(F32)
+    grads = weights.reshape(4, C, C).astype(F32)
     return (out.reshape(48, 16, C), grad_features, grads[0], grads[1], grads[2], grads[3])
 
 

time: 165 us -> 161 us (0.976)
  local copies, waits for them, and re-layouts: 8.93 us -> 4.21 us
    pallas_call x1 -> x0, Pallas kernels: 29.7 us -> none  [gather_call(): pl.pallas_call(gather_kernel, out_shape=(jax.ShapeDtypeStruct((48, 16, C)...]
    pallas_call x1, Pallas kernels: 61.9 us -> 90.9 us  [main_call(): pl.pallas_call(main_kernel, out_shape=(jax.ShapeDtypeStruct((NT, C), BF16...]
    slice x5 -> x0, local copies, waits for them, and re-layouts: 3.53 us -> none  [the longest x2 1.1 us: body(): grads[3]]
    unnamed x8 -> x7, local copies, waits for them, and re-layouts: 5.2 us -> 1.93 us
    squeeze x0 -> x1, local copies, waits for them, and re-layouts: none -> 2.08 us  [body(): grads[3]]
where the time goes in v2:
time: 161 us; the launch traced here: 159 us
  Pallas kernels  151 us (94%)
  local copies, waits for them, and re-layouts  4.21 us (3%)
  other arithmetic  2.61 us (2%)
    pallas_call x1, Pallas kernels, main_call(): pl.pallas_call(main_kernel, out_shape=(jax.ShapeDtypeStruct((NT, C), BF16...  90.9 us
    pallas_call x1, Pallas kernels, reduce_call(): pl.pallas_call(reduce_kernel, out_shape=(jax.ShapeDtypeStruct((12, C), F3...  60.5 us

profile of v2, /device:TPU:1, one launch (start us, length us, event | category | flops | bytes accessed | tf_op | source)
XLA Modules:
  0.0 158.9 jit_solution(6984866086350362555)
XLA Ops:
  0.6 90.9 %attention.1 = (bf16[768,512]{1,0:T(8,128)(2,1)}, f32[768,512]{1,0:T(8,128)}, bf16[1536,512]{1,0:T(8,128)(2,1)}, bf16[2048,512]{1,0:T(8,128)(2,1)}) custom-call(bf16[48,16,512]{2,1,0:T(8,128)(2,1)} %f_ref.1, bf16[768,512]{1,0:T(8,128)(2,1)} %bitcast.21, bf16[512,512]{1,0:T(8,128)(2,1)} %wq_ref.1, bf16[512,512]{1,0:T(8,128)(2,1)} %wk_ref.1, ...), custom_call_target="tpu_custom_call" | custom-call | tf_op jit(solution)/shard_map/attention/pallas_call | solution.py:142
  91.5 60.5 %reduce.1 = (f32[12,512]{1,0:T(8,128)}, bf16[2,64,16,512]{3,2,1,0:T(8,128)(2,1)}) custom-call(bf16[64,24,512]{2,1,0:T(8,128)(2,1)} %bitcast.19, bf16[2,64,16,512]{3,2,1,0:T(8,128)(2,1)} %bitcast.18), custom_call_target="tpu_custom_call" | custom-call | tf_op jit(solution)/shard_map/reduce/pallas_call | solution.py:325
  152.0 0.0 copy-start.1
  152.0 0.9 broadcast_multiply_fusion
  152.9 0.2 broadcast_in_dim.8
  153.1 0.3 copy-done.1
  153.4 0.0 copy-start
  153.4 1.2 add_convert_fusion
  154.6 0.7 copy-done
  155.3 0.6 convert.1
  155.9 0.0 copy-start.2
  155.9 2.1 %slice_bitcast_fusion = (f32[512,512]{1,0:T(8,128)}, f32[512,512]{1,0:T(8,128)}, f32[512,512]{1,0:T(8,128)}, f32[512,512]{1,0:T(8,128)}) fusion(f32[4,512,512]{2,1,0:T(8,128)S(1)} %convert.1), kind=kLoop, calls=%fused_computation.1 | loop fusion | bytes 8388608 | tf_op jit(solution)/shard_map/squeeze | solution.py:348
  158.0 0.0 copy-done.2
  158.0 0.9 copy.13
  (1 shorter events, 0.0 us)
Async XLA Ops:
  152.0 1.4 copy-start.1
  153.4 1.9 %copy-start = (bf16[2,64,16,512]{3,2,1,0:T(8,128)(2,1)S(1)}, bf16[2,64,16,512]{3,2,1,0:T(8,128)(2,1)}, u32[]{:S(2)}) copy-start(bf16[2,64,16,512]{3,2,1,0:T(8,128)(2,1)} %get-tuple-element.17) | copy-start | bytes 6291460
  155.9 2.1 %copy-start.2 = (bf16[768,512]{1,0:T(8,128)(2,1)S(1)}, bf16[768,512]{1,0:T(8,128)(2,1)}, u32[]{:S(2)}) copy-start(bf16[768,512]{1,0:T(8,128)(2,1)} %get-tuple-element.12) | copy-start | bytes 2359300
